TPU v7x, 32 devices: a whole 2x2x4 slice. The times are simulated.
32 devices in a mesh: seq: 8 (over y, x, core), wshard: 4 (over z).
Axes of the slice: x: 2, y: 2, z: 4, core: 2. Of those that a mesh axis runs over, the one named last changes fastest.
Arguments:
- block_in: bfloat16 [4, 2048, 1536], P('wshard', 'seq'), may hold values from -6 to 6
- cotangent: bfloat16 [4, 2048, 1536], P('wshard', 'seq'), may hold values from -6 to 6
- in_weight: float32 [1536, 6448], P(('seq', 'wshard')), may hold values from -0.15625 to 0.15625
- out_weight: float32 [3072, 1536], P(('seq', 'wshard')), may hold values from -0.109375 to 0.109375
- in_gain: float32 [1536], replicated, may hold values from 0.5 to 1.5
- out_gain: float32 [3072], replicated, may hold values from 0.5 to 1.5
- conv_inner: float32 [5, 3072], replicated, may hold values from -3 to 3
- conv_shared: float32 [5, 256], replicated, may hold values from -3 to 3
- head_params: float32 [3, 48], replicated, may hold values from -5 to 1.5, as said below
- first_in_weight: float32 [1536, 6448], P(('seq', 'wshard')), may hold values from -6 to 6
- first_out_weight: float32 [3072, 1536], P(('seq', 'wshard')), may hold values from -6 to 6
- first_in_gain: float32 [1536], replicated, may hold values from -6 to 6
- first_out_gain: float32 [3072], replicated, may hold values from -6 to 6
- first_conv_inner: float32 [5, 3072], replicated, may hold values from -6 to 6
- first_conv_shared: float32 [5, 256], replicated, may hold values from -6 to 6
- first_head_params: float32 [3, 48], replicated, may hold values from -6 to 6
- second_in_weight: float32 [1536, 6448], P(('seq', 'wshard')), may hold values from 0.01 to 1
- second_out_weight: float32 [3072, 1536], P(('seq', 'wshard')), may hold values from 0.01 to 1
- second_in_gain: float32 [1536], replicated, may hold values from 16.384 to 1638.4
- second_out_gain: float32 [3072], replicated, may hold values from 0.01 to 1
- second_conv_inner: float32 [5, 3072], replicated, may hold values from 0.01 to 1
- second_conv_shared: float32 [5, 256], replicated, may hold values from 0.01 to 1
- second_head_params: float32 [3, 48], replicated, may hold values from 0.01 to 1
Outputs:
- block_out: float32 [4, 2048, 1536], P('wshard', 'seq')
- grad_in: float32 [4, 2048, 1536], P('wshard', 'seq')
- grad_in_weight: float32 [1536, 6448], P(('seq', 'wshard'))
- grad_out_weight: float32 [3072, 1536], P(('seq', 'wshard'))
- grad_in_gain: float32 [1536], replicated
- grad_out_gain: float32 [3072], replicated
- grad_conv_inner: float32 [5, 3072], replicated
- grad_conv_shared: float32 [5, 256], replicated
- grad_head_params: float32 [3, 48], replicated
- new_in_weight: float32 [1536, 6448], P(('seq', 'wshard'))
- new_out_weight: float32 [3072, 1536], P(('seq', 'wshard'))
- updated_input_gain: float32 [1536], replicated
- new_out_gain: float32 [3072], replicated
- new_conv_inner: float32 [5, 3072], replicated
- new_conv_shared: float32 [5, 256], replicated
- new_head_params: float32 [3, 48], replicated
- new_first_in_weight: float32 [1536, 6448], P(('seq', 'wshard'))
- new_first_out_weight: float32 [3072, 1536], P(('seq', 'wshard'))
- new_first_in_gain: float32 [1536], replicated
- new_first_out_gain: float32 [3072], replicated
- new_first_conv_inner: float32 [5, 3072], replicated
- new_first_conv_shared: float32 [5, 256], replicated
- updated_head_first_moment: float32 [3, 48], replicated
- new_second_in_weight: float32 [1536, 6448], P(('seq', 'wshard'))
- new_second_out_weight: float32 [3072, 1536], P(('seq', 'wshard'))
- new_second_in_gain: float32 [1536], replicated
- new_second_out_gain: float32 [3072], replicated
- new_second_conv_inner: float32 [5, 3072], replicated
- new_second_conv_shared: float32 [5, 256], replicated
- new_second_head_params: float32 [2, 48], replicated
- new_second_skip: float32 [48], replicated
Inputs may be any that keep to these rules, and one draw needn't show every extreme that they name: `head_params`: row 0 holds step biases, row 1 logarithms of decay rates, row 2 skip gains.
All inputs are finite; a program needn't handle non-finite values.
Results may differ from a plain program's by a relative error of at most 0.02.
The roundings to bfloat16 on the way count: a program that leaves them out, or rounds other values in their place, can miss the bound.
Values may be sent and summed in bfloat16 or wider, within the bound.
A program may use at most 256 MiB of HBM per device.

v0:
```python
import jax
import jax.numpy as jnp
from jax import lax
from jax.sharding import PartitionSpec as P

P_SIZE = 64
N_STATE = 128
BLOCK_LEN = 256
E = 3072
norm_eps = 1e-05
beta_one = 0.9
beta_two = 0.95
adam_eps = 1e-08
adam_step = 3.0
weight_learning_rate = 0.01
matrix_decay = 0.1
small_rate = 0.1


def causal_conv(values, taps):
    length = values.shape[1]
    width = taps.shape[0] - 1
    padded = jnp.pad(values, ((0, 0), (width - 1, 0), (0, 0)))
    total = taps[width] + taps[0] * padded[:, 0:length]
    for shift in range(1, width):
        total = total + taps[shift] * padded[:, shift : shift + length]
    return total


def block_step(state, inputs):
    inner_part, step_part, learning_rate_piece, b_part, c_part = inputs
    high = lax.Precision.HIGHEST
    cumul = jnp.cumsum(learning_rate_piece, axis=1)
    scores = jnp.einsum("sin,sjn->sij", c_part, b_part, precision=high)
    rows = lax.broadcasted_iota(jnp.int32, (BLOCK_LEN, BLOCK_LEN), 0)
    cols = lax.broadcasted_iota(jnp.int32, (BLOCK_LEN, BLOCK_LEN), 1)
    lower = (rows >= cols)[None, :, :, None]
    spread = cumul[:, :, None, :] - cumul[:, None, :, :]
    decay = jnp.where(lower, jnp.exp(jnp.where(lower, spread, 0.0)), 0.0)
    weights = scores[..., None] * decay * step_part[:, None, :, :]
    within = jnp.einsum("sijh,sjhp->sihp", weights, inner_part, precision=high)
    carried = (
        jnp.einsum("sin,shpn->sihp", c_part, state, precision=high) * jnp.exp(cumul)[..., None]
    )
    tail = jnp.exp(cumul[:, -1:, :] - cumul) * step_part
    fresh = jnp.einsum("sjn,sjh,sjhp->shpn", b_part, tail, inner_part, precision=high)
    new_state = jnp.exp(cumul[:, -1, :])[:, :, None, None] * state + fresh
    return (new_state, within + carried)


def state_space(inner, step, rate, b_mat, c_mat):
    batch, length, heads, head_size = inner.shape
    blocks = length // BLOCK_LEN

    def blockify(values):
        return jnp.moveaxis(values.reshape((batch, blocks, BLOCK_LEN) + values.shape[2:]), 1, 0)

    start = jnp.zeros((batch, heads, head_size, b_mat.shape[2]), dtype=inner.dtype)
    _, outputs = lax.scan(
        jax.checkpoint(block_step),
        start,
        (blockify(inner), blockify(step), blockify(rate), blockify(b_mat), blockify(c_mat)),
    )
    return jnp.moveaxis(outputs, 0, 1).reshape(batch, length, heads, head_size)


def mixer(gate_inner, shared, step_raw, conv_local, conv_common, head_local):
    batch, length = (gate_inner.shape[0], gate_inner.shape[1])
    heads = step_raw.shape[2]
    parts = gate_inner.reshape(batch, length, heads, 2, P_SIZE)
    gate_vals = parts[:, :, :, 0, :].reshape(batch, length, heads * P_SIZE)
    inner_vals = parts[:, :, :, 1, :].reshape(batch, length, heads * P_SIZE)
    inner_act = jax.nn.silu(causal_conv(inner_vals, conv_local))
    shared_act = jax.nn.silu(causal_conv(shared, conv_common))
    half = shared.shape[2] // 2
    step = jax.nn.softplus(step_raw + head_local[0])
    rate = -step * jnp.exp(head_local[1])
    inner_heads = inner_act.reshape(batch, length, heads, P_SIZE)
    output = state_space(inner_heads, step, rate, shared_act[..., :half], shared_act[..., half:])
    output = output + head_local[2][:, None] * inner_heads
    return output.reshape(batch, length, heads * P_SIZE) * jax.nn.silu(gate_vals)


def adamw(param, grad, first, second_moment, rate, decay):
    first_new = beta_one * first + (1.0 - beta_one) * grad
    second_new = beta_two * second_moment + (1.0 - beta_two) * grad * grad
    corrected = (
        first_new
        / (1.0 - beta_one**adam_step)
        / (jnp.sqrt(second_new / (1.0 - beta_two**adam_step)) + adam_eps)
    )
    return (param - rate * (corrected + decay * param), first_new, second_new)


def local(
    block_in,
    cotangent,
    in_weight,
    out_weight,
    in_gain,
    out_gain,
    conv_inner,
    conv_shared,
    head_params,
    first_in_weight,
    first_out_weight,
    first_in_gain,
    first_out_gain,
    first_conv_inner,
    first_conv_shared,
    first_head_params,
    second_in_weight,
    second_out_weight,
    second_in_gain,
    second_out_gain,
    second_conv_inner,
    second_conv_shared,
    second_head_params,
):
    seq_index = lax.axis_index("seq")
    inputs = block_in.astype(jnp.float32)
    rms_in = lax.rsqrt(jnp.mean(inputs * inputs, axis=-1, keepdims=True) + norm_eps)
    normed = (inputs * rms_in * in_gain).astype(jnp.bfloat16)
    in_w16 = in_weight.astype(jnp.bfloat16)
    out_w16 = out_weight.astype(jnp.bfloat16)
    column_list = normed
    projected = jnp.einsum(
        "fbe,ek->fbk",
        column_list,
        lax.all_gather(in_w16, ("seq", "wshard"), axis=0, tiled=True),
        preferred_element_type=jnp.float32,
    ).astype(jnp.bfloat16)
    gate_inner = projected[:, :, : 2 * E]
    shared = projected[:, :, 2 * E : 2 * E + 2 * N_STATE]
    step_raw = projected[:, :, 2 * E + 2 * N_STATE :]
    head_gate, head_step = (
        lax.all_to_all(gate_inner, "seq", split_axis=2, concat_axis=1, tiled=True),
        lax.all_to_all(step_raw, "seq", split_axis=2, concat_axis=1, tiled=True),
    )
    head_shared = lax.all_gather(shared, "seq", axis=1, tiled=True)
    heads_dev = head_step.shape[2]
    inner_start = seq_index * (heads_dev * P_SIZE)
    conv_local = lax.dynamic_slice_in_dim(conv_inner, inner_start, heads_dev * P_SIZE, 1)
    head_local = lax.dynamic_slice_in_dim(head_params, seq_index * heads_dev, heads_dev, 1)
    gated, mixer_back = jax.vjp(
        mixer,
        head_gate.astype(jnp.float32),
        head_shared.astype(jnp.float32),
        head_step.astype(jnp.float32),
        conv_local,
        conv_shared,
        head_local,
    )
    gated32 = lax.all_to_all(
        gated.astype(jnp.bfloat16), "seq", split_axis=1, concat_axis=2, tiled=True
    ).astype(jnp.float32)
    rms_out = lax.rsqrt(jnp.mean(gated32 * gated32, axis=-1, keepdims=True) + norm_eps)
    gnormed = (gated32 * rms_out * out_gain).astype(jnp.bfloat16)
    column_list = gnormed
    mixed = jnp.einsum(
        "brg,ga->bra",
        column_list,
        lax.all_gather(out_w16, ("seq", "wshard"), axis=0, tiled=True),
        preferred_element_type=jnp.float32,
    )
    d_gnormed = jnp.einsum(
        "oum,am->oua",
        cotangent,
        lax.all_gather(out_w16, ("seq", "wshard"), axis=0, tiled=True),
        preferred_element_type=jnp.float32,
    )
    block_out = inputs + mixed
    d_out_gain = jnp.sum(d_gnormed * gated32 * rms_out, axis=(0, 1))
    scaled = d_gnormed * out_gain
    d_gated = (
        rms_out * scaled - gated32 * rms_out**3 * jnp.mean(scaled * gated32, axis=-1, keepdims=True)
    ).astype(jnp.bfloat16)
    head_cotan = lax.all_to_all(d_gated, "seq", split_axis=2, concat_axis=1, tiled=True).astype(
        jnp.float32
    )
    d_gate, d_shared, d_step, d_conv_local, d_common, d_head_local = mixer_back(head_cotan)
    tok_gate, tok_step = (
        lax.all_to_all(d_gate.astype(jnp.bfloat16), "seq", split_axis=1, concat_axis=2, tiled=True),
        lax.all_to_all(d_step.astype(jnp.bfloat16), "seq", split_axis=1, concat_axis=2, tiled=True),
    )
    shared_sum = lax.psum_scatter(
        d_shared.astype(jnp.bfloat16), "seq", scatter_dimension=1, tiled=True
    )
    projected_gradient = jnp.concatenate([tok_gate, shared_sum, tok_step], axis=2)
    d_normed = jnp.einsum(
        "ozu,hu->ozh",
        projected_gradient,
        lax.all_gather(in_w16, ("seq", "wshard"), axis=0, tiled=True),
        preferred_element_type=jnp.float32,
    )
    d_in_gain = jnp.sum(d_normed * inputs * rms_in, axis=(0, 1))
    scaled_in = d_normed * in_gain
    grad_in = (
        cotangent.astype(jnp.float32)
        + rms_in * scaled_in
        - inputs * rms_in**3 * jnp.mean(scaled_in * inputs, axis=-1, keepdims=True)
    )
    d_conv_full = lax.dynamic_update_slice_in_dim(
        jnp.zeros_like(conv_inner), d_conv_local, inner_start, 1
    )
    d_head_full = lax.dynamic_update_slice_in_dim(
        jnp.zeros_like(head_params), d_head_local, seq_index * heads_dev, 1
    )
    grad_in_gain, grad_out_gain, grad_conv_inner, grad_conv_shared, grad_head_params = lax.psum(
        (d_in_gain, d_out_gain, d_conv_full, d_common, d_head_full), ("seq", "wshard")
    )
    column_list = normed
    grad_in_weight = lax.psum_scatter(
        jnp.einsum(
            "nkm,nkc->mc", column_list, projected_gradient, preferred_element_type=jnp.float32
        ),
        ("seq", "wshard"),
        scatter_dimension=0,
        tiled=True,
    )
    column_list = gnormed
    grad_out_weight = lax.psum_scatter(
        jnp.einsum("kcb,kch->bh", column_list, cotangent, preferred_element_type=jnp.float32),
        ("seq", "wshard"),
        scatter_dimension=0,
        tiled=True,
    )
    new_in_weight, new_first_in_weight, new_second_in_weight = adamw(
        in_weight,
        grad_in_weight,
        first_in_weight,
        second_in_weight,
        weight_learning_rate,
        matrix_decay,
    )
    new_out_weight, new_first_out_weight, new_second_out_weight = adamw(
        out_weight,
        grad_out_weight,
        first_out_weight,
        second_out_weight,
        weight_learning_rate,
        matrix_decay,
    )
    updated_input_gain, new_first_in_gain, new_second_in_gain = adamw(
        in_gain, grad_in_gain, first_in_gain, second_in_gain, small_rate, 0.0
    )
    new_out_gain, new_first_out_gain, new_second_out_gain = adamw(
        out_gain, grad_out_gain, first_out_gain, second_out_gain, small_rate, 0.0
    )
    new_conv_inner, new_first_conv_inner, new_second_conv_inner = adamw(
        conv_inner, grad_conv_inner, first_conv_inner, second_conv_inner, small_rate, 0.0
    )
    new_conv_shared, new_first_conv_shared, new_second_conv_shared = adamw(
        conv_shared, grad_conv_shared, first_conv_shared, second_conv_shared, small_rate, 0.0
    )
    new_head_params, updated_head_first_moment, head_second_all = adamw(
        head_params, grad_head_params, first_head_params, second_head_params, small_rate, 0.0
    )
    return (
        block_out,
        grad_in,
        grad_in_weight,
        grad_out_weight,
        grad_in_gain,
        grad_out_gain,
        grad_conv_inner,
        grad_conv_shared,
        grad_head_params,
        new_in_weight,
        new_out_weight,
        updated_input_gain,
        new_out_gain,
        new_conv_inner,
        new_conv_shared,
        new_head_params,
        new_first_in_weight,
        new_first_out_weight,
        new_first_in_gain,
        new_first_out_gain,
        new_first_conv_inner,
        new_first_conv_shared,
        updated_head_first_moment,
        new_second_in_weight,
        new_second_out_weight,
        new_second_in_gain,
        new_second_out_gain,
        new_second_conv_inner,
        new_second_conv_shared,
        head_second_all[0:2],
        head_second_all[2],
    )


def solution(mesh):
    return jax.shard_map(
        local,
        mesh=mesh,
        in_specs=(
            P("wshard", "seq", None),
            P("wshard", "seq", None),
            P(("seq", "wshard"), None),
            P(("seq", "wshard"), None),
            P(),
            P(),
            P(),
            P(),
            P(),
            P(("seq", "wshard"), None),
            P(("seq", "wshard"), None),
            P(),
            P(),
            P(),
            P(),
            P(),
            P(("seq", "wshard"), None),
            P(("seq", "wshard"), None),
            P(),
            P(),
            P(),
            P(),
            P(),
        ),
        out_specs=(
            P("wshard", "seq", None),
            P("wshard", "seq", None),
            P(("seq", "wshard"), None),
            P(("seq", "wshard"), None),
            P(),
            P(),
            P(),
            P(),
            P(),
            P(("seq", "wshard"), None),
            P(("seq", "wshard"), None),
            P(),
            P(),
            P(),
            P(),
            P(),
            P(("seq", "wshard"), None),
            P(("seq", "wshard"), None),
            P(),
            P(),
            P(),
            P(),
            P(),
            P(("seq", "wshard"), None),
            P(("seq", "wshard"), None),
            P(),
            P(),
            P(),
            P(),
            P(),
            P(),
        ),
        check_vma=False,
    )
```

profile of v0, /device:TPU:0, one launch (start us, length us, event | category | flops | bytes accessed | tf_op | source)
XLA Modules:
  0.0 2023.6 jit_solution(13329375079531035761)
XLA Ops:
  11.6 132.1 %all-gather.4.cloned.1.call-done = bf16[1536,6448]{1,0:T(8,128)(2,1)} async-done(((bf16[48,6448]{1,0:T(8,128)(2,1)}), bf16[1536,6448]{1,0:T(8,128)(2,1)}) %all-gather.4.cloned.1.call-update) | async-done | bytes 19808272 | tf_op jit(solution)/shard_map/all_gather | solution.py:130
  143.6 14.0 fusion.107
  167.6 37.2 %copy.613 = bf16[1,256,6144]{1,0,2:T(2,128)(2,1)} copy(bf16[1,256,6144]{1,2,0:T(8,128)(2,1)S(1)} %slice.200) | data formatting | bytes 6291456 | tf_op jit(solution)/shard_map/slice | solution.py:133
  204.9 31.5 %reduce.89 = bf16[6144,256]{1,0:T(8,128)(2,1)S(1)} reduce(bf16[6144,1,256]{2,1,0:T(2,128)(2,1)} %bitcast.657, bf16[]{:T(256)} %broadcast.1020), dimensions={1}, to_apply=%bitcast.470.reduce_sub_computation | reduce | bytes 6291458
  240.0 4.6 all-to-all-start.1
  259.4 23.1 %all-to-all-done.1 = bf16[8,2,98304]{2,1,0:T(2,128)(2,1)S(1)} async-done(((bf16[8,2,98304]{2,1,0:T(2,128)(2,1)}), bf16[8,2,98304]{2,1,0:T(2,128)(2,1)S(1)}, u32[]{:S(2)}, u32[]{:S(2)}) %all-to-all-start.1) | async-done | bytes 3145760 | tf_op jit(solution)/shard_map/all_to_all | solution.py:137
  282.4 5.3 reshape.1694
  287.7 9.1 copy.611
  296.8 7.1 reshape.1633
  307.2 4.5 fusion.118
  317.7 185.0 %while.44 = (s32[]{:T(128)}, f32[1,6,64,128]{3,2,1,0:T(8,128)S(1)}, f32[8,1,256,6,64]{2,0,4,3,1:T(8,128)}, f32[8,1,6,64,128]{4,3,2,1,0:T(8,128)}, f32[8,1,256,6]...) while((s32[]{:T(128)}, f32[1,6,64,128]{3,2,1,0:T(8,128)S(1)}, ...), condition=%wide.region_4.5_spmd.clone.clone, body=%wide.region_1.4_spmd.clone.clone.sunk | while | flops 707349504 | bytes 5805416 | solution.py:59
  331.4 9.8 dynamic_update_slice.95
  354.5 9.8 dynamic_update_slice.95
  377.6 9.8 dynamic_update_slice.95
  400.6 9.8 dynamic_update_slice.95
  423.7 9.8 dynamic_update_slice.95
  446.7 9.8 dynamic_update_slice.95
  469.8 9.8 dynamic_update_slice.95
  492.8 9.8 dynamic_update_slice.95
  502.7 4.6 transpose.193
  507.3 4.8 multiply_convert_fusion.1
  512.0 8.5 copy.488
  520.5 35.5 %reduce.90 = bf16[2048,384]{1,0:T(8,128)(2,1)} reduce(bf16[2048,1,384]{2,1,0:T(2,128)(2,1)} %bitcast.669, bf16[]{:T(256)} %broadcast.1020), dimensions={1}, to_apply=%bitcast.432.reduce_sub_computation | reduce | bytes 3145730
  559.7 4.3 all-to-all-start.2
  564.1 20.9 %all-to-all-done.2 = bf16[8,2,49152]{2,1,0:T(2,128)(2,1)} async-done(((bf16[8,2,49152]{2,1,0:T(2,128)(2,1)}), bf16[8,2,49152]{2,1,0:T(2,128)(2,1)}, u32[]{:S(2)}, u32[]{:S(2)}) %all-to-all-start.2) | async-done | bytes 1572896 | tf_op jit(solution)/shard_map/all_to_all | solution.py:154
  585.1 6.5 reshape.1696
  600.2 10.7 fusion.139
  610.9 204.3 %reduce-scatter.8.cloned.1.call-done = f32[96,1536]{1,0:T(8,128)} async-done(((f32[3072,1536]{1,0:T(8,128)}), f32[96,1536]{1,0:T(8,128)}) %reduce-scatter.8.cloned.1.call-update) | async-done | bytes 589840 | tf_op jit(solution)/shard_map/reduce_scatter | solution.py:222
  822.5 76.8 %all-gather.8.cloned.1.call-done = bf16[3072,1536]{1,0:T(8,128)(2,1)} async-done(((bf16[96,1536]{1,0:T(8,128)(2,1)}), bf16[3072,1536]{1,0:T(8,128)(2,1)}) %all-gather.8.cloned.1.call-update) | async-done | bytes 9437200 | tf_op jit(solution)/shard_map/all_gather | solution.py:163
  899.3 8.4 multiply_reduce_fusion.7
  910.0 7.6 copy.491
  917.6 17.8 reduce.91
  947.2 17.2 all-to-all-done.3
  964.4 4.7 reshape.1698
  981.4 355.6 %while.43 = (s32[]{:T(128)}, f32[1,6,64,128]{3,2,1,0:T(8,128)S(1)}, f32[8,1,256,6,64]{2,0,4,3,1:T(8,128)}, f32[8,1,256,6]{3,2,1,0:T(8,128)}, f32[8,1,256,6]{2,0,...) while((s32[]{:T(128)}, f32[1,6,64,128]{3,2,1,0:T(8,128)S(1)}, ...), condition=%wide.region_19.20_spmd.clone, body=%wide.region_7.19_spmd.clone.sunk | while | flops 1670419456 | bytes 15714059 | solution.py:59
  999.2 9.8 dynamic_update_slice.91
  1009.9 7.6 reduce-window.74
  1043.6 9.8 dynamic_update_slice.91
  1054.3 7.6 reduce-window.74
  1088.0 9.8 dynamic_update_slice.91
  1098.7 7.6 reduce-window.74
  1132.4 9.8 dynamic_update_slice.91
  1143.1 7.6 reduce-window.74
  1176.8 9.8 dynamic_update_slice.91
  1187.5 7.6 reduce-window.74
  1221.2 9.8 dynamic_update_slice.91
  1231.9 7.6 reduce-window.74
  1265.6 9.8 dynamic_update_slice.91
  1276.3 7.6 reduce-window.74
  1310.0 9.8 dynamic_update_slice.91
  1320.7 7.6 reduce-window.74
  1341.8 11.5 reduce.92
  1358.1 4.8 transpose.194
  1369.0 12.4 multiply_reduce_fusion.6
  1392.1 15.7 copy.509
  1407.8 31.6 %reduce.93 = bf16[2048,768]{1,0:T(8,128)(2,1)S(1)} reduce(bf16[2048,1,768]{2,1,0:T(2,128)(2,1)} %bitcast.656, bf16[]{:T(256)} %broadcast.1020), dimensions={1}, to_apply=%bitcast.438.reduce_sub_computation | reduce | bytes 6291458
  1443.0 4.7 all-to-all-start.4
  1460.7 27.7 %all-to-all-done.4 = bf16[8,2,98304]{2,1,0:T(2,128)(2,1)} async-done(((bf16[8,2,98304]{2,1,0:T(2,128)(2,1)}), bf16[8,2,98304]{2,1,0:T(2,128)(2,1)}, u32[]{:S(2)}, u32[]{:S(2)}) %all-to-all-start.4) | async-done | bytes 3145760 | tf_op jit(solution)/shard_map/all_to_all | solution.py:183
  1488.4 7.8 reshape.1702
  1502.4 12.5 fusion.132
  1515.0 18.5 fusion.135
  1535.5 7.8 convert_add_fusion
  1545.1 94.3 %all-reduce.32.cloned.1.call-done = (f32[1536]{0:T(1024)}, f32[3072]{0:T(1024)}, f32[5,3072]{1,0:T(8,128)}, f32[5,256]{1,0:T(8,128)}, f32[3,48]{1,0:T(4,128)}) async-done(((f32[1536]{0:T(1024)}, f32[3072]{0:T(1024)}, f32[5,3072]{1,0:T(8,128)}, f32[5,256]{1,0:T(8,128)}, f32[3,48]{1,0:T(4,128)}), (f32[1536]{0:T(1024)}, f32[3072]{0:T(1024)}, f32[5,3072]{1,0:T(8,128)}, f32[5,256]{1,0:T(8,128)}, ...) | async-done | bytes 85584 | tf_op jit(solution)/shard_map/psum | solution.py:209
  1647.4 361.7 %reduce-scatter.6.cloned.1.call-done = f32[48,6448]{1,0:T(8,128)} async-done(((f32[1536,6448]{1,0:T(8,128)}), f32[48,6448]{1,0:T(8,128)}) %reduce-scatter.6.cloned.1.call-update) | async-done | bytes 1238032 | tf_op jit(solution)/shard_map/reduce_scatter | solution.py:213
  (923 shorter events, 474.9 us)
Async XLA Ops:
  7.2 136.4 %copy-start.11 = (bf16[1,256,1536]{2,1,0:T(8,128)(2,1)S(1)}, bf16[1,256,1536]{2,1,0:T(8,128)(2,1)}, u32[]{:S(2)}) copy-start(bf16[1,256,1536]{2,1,0:T(8,128)(2,1)} %param.27) | copy-start | bytes 2359300
  7.2 136.4 %copy-start.26 = (f32[1536]{0:T(1024)S(1)}, f32[1536]{0:T(1024)}, u32[]{:S(2)}) copy-start(f32[1536]{0:T(1024)} %param.31) | copy-start | bytes 18436
  7.2 136.4 %all-gather.4.cloned.1.call-start = ((), (), s32[]{:S(2)}) async-start(), calls=%async_computation.9 | async-start | bytes 20680704 | tf_op jit(solution)/shard_map/all_gather | solution.py:130
  9.6 238.6 %all-gather.6.cloned.1.call-start = ((), (), s32[]{:S(2)}) async-start(), calls=%async_computation.10 | async-start | bytes 1179648 | tf_op jit(solution)/shard_map/all_gather | solution.py:140
  11.6 146.1 %copy-start.48 = (f32[256]{0:T(256)}, f32[256]{0:T(256)S(1)}, u32[]{:S(2)}) copy-start(f32[256]{0:T(256)S(1)} %get-tuple-element.934) | copy-start | bytes 3076
  162.0 78.0 %all-to-all-start = ((bf16[8,2,768]{2,1,0:T(2,128)(2,1)}), bf16[8,2,768]{2,1,0:T(2,128)(2,1)S(1)}, u32[]{:S(2)}, u32[]{:S(2)}) async-start(bf16[8,2,768]{2,1,0:T(2,128)(2,1)} %reshape.1691), calls=%async_computation | async-start | bytes 49152 | tf_op jit(solution)/shard_map/all_to_all | solution.py:138
  240.0 42.4 %all-to-all-start.1 = ((bf16[8,2,98304]{2,1,0:T(2,128)(2,1)}), bf16[8,2,98304]{2,1,0:T(2,128)(2,1)S(1)}, u32[]{:S(2)}, u32[]{:S(2)}) async-start(bf16[8,2,98304]{2,1,0:T(2,128)(2,1)} %reshape.1693), calls=%async_computation.1 | async-start | bytes 6291456 | tf_op jit(solution)/shard_map/all_to_all | solution.py:137
  244.9 262.4 %copy-start.46 = (f32[384]{0:T(512)}, f32[384]{0:T(512)S(1)}, u32[]{:S(2)}) copy-start(f32[384]{0:T(512)S(1)} %mul.1143) | copy-start | bytes 4612
  245.9 61.3 %copy-start.38 = (f32[384]{0:T(512)}, f32[384]{0:T(512)S(1)}, u32[]{:S(2)}) copy-start(f32[384]{0:T(512)S(1)} %get-tuple-element.804) | copy-start | bytes 4612
  245.9 61.3 %copy-start.40 = (f32[384]{0:T(512)}, f32[384]{0:T(512)S(1)}, u32[]{:S(2)}) copy-start(f32[384]{0:T(512)S(1)} %get-tuple-element.805) | copy-start | bytes 4612
  245.9 61.3 %copy-start.42 = (f32[384]{0:T(512)}, f32[384]{0:T(512)S(1)}, u32[]{:S(2)}) copy-start(f32[384]{0:T(512)S(1)} %get-tuple-element.806) | copy-start | bytes 4612
  245.9 61.3 %copy-start.44 = (f32[384]{0:T(512)}, f32[384]{0:T(512)S(1)}, u32[]{:S(2)}) copy-start(f32[384]{0:T(512)S(1)} %get-tuple-element.807) | copy-start | bytes 4612
  307.2 636.9 %copy-start = (f32[1,2048,6,1,64]{1,4,3,2,0:T(8,128)}, f32[1,2048,6,1,64]{1,4,3,2,0:T(8,128)S(1)}, u32[]{:S(2)}) copy-start(f32[1,2048,6,1,64]{1,4,3,2,0:T(8,128)S(1)} %get-tuple-element.912) | copy-start | bytes 9437188
  559.7 25.3 %all-to-all-start.2 = ((bf16[8,2,49152]{2,1,0:T(2,128)(2,1)}), bf16[8,2,49152]{2,1,0:T(2,128)(2,1)}, u32[]{:S(2)}, u32[]{:S(2)}) async-start(bf16[8,2,49152]{2,1,0:T(2,128)(2,1)} %reshape.1695), calls=%async_computation.2 | async-start | bytes 3145728 | tf_op jit(solution)/shard_map/all_to_all | solution.py:154
  564.1 251.1 %reduce-scatter.8.cloned.1.call-start = ((), (), s32[]{:S(2)}) async-start(), calls=%async_computation.14 | async-start | bytes 19464192 | tf_op jit(solution)/shard_map/reduce_scatter | solution.py:222
  595.9 311.8 %copy-start.60 = (f32[256]{0:T(256)}, f32[256]{0:T(256)S(1)}, u32[]{:S(2)}) copy-start(f32[256]{0:T(256)S(1)} %get-tuple-element.936) | copy-start | bytes 3076
  610.9 288.4 %all-gather.8.cloned.1.call-start = ((), (), s32[]{:S(2)}) async-start(), calls=%async_computation.11 | async-start | bytes 9732096 | tf_op jit(solution)/shard_map/all_gather | solution.py:163
  939.1 25.3 %all-to-all-start.3 = ((bf16[8,2,49152]{2,1,0:T(2,128)(2,1)}), bf16[8,2,49152]{2,1,0:T(2,128)(2,1)}, u32[]{:S(2)}, u32[]{:S(2)}) async-start(bf16[8,2,49152]{2,1,0:T(2,128)(2,1)} %reshape.1697), calls=%async_computation.3 | async-start | bytes 3145728 | tf_op jit(solution)/shard_map/all_to_all | solution.py:178
  996.4 12.7 copy-start.24
  998.7 27.5 %copy-start.14 = (f32[1,6,64,128]{3,2,1,0:T(8,128)S(1)}, f32[1,6,64,128]{3,2,1,0:T(8,128)}, u32[]{:S(2)}) copy-start(f32[1,6,64,128]{3,2,1,0:T(8,128)} %fusion.229) | copy-start | bytes 589828 | tf_op jit(solution)/shard_map/transpose(jvp())/while
  1040.8 12.7 copy-start.24
  1043.1 27.5 %copy-start.14 = (f32[1,6,64,128]{3,2,1,0:T(8,128)S(1)}, f32[1,6,64,128]{3,2,1,0:T(8,128)}, u32[]{:S(2)}) copy-start(f32[1,6,64,128]{3,2,1,0:T(8,128)} %fusion.229) | copy-start | bytes 589828 | tf_op jit(solution)/shard_map/transpose(jvp())/while
  1085.2 12.7 copy-start.24
  1087.5 27.5 %copy-start.14 = (f32[1,6,64,128]{3,2,1,0:T(8,128)S(1)}, f32[1,6,64,128]{3,2,1,0:T(8,128)}, u32[]{:S(2)}) copy-start(f32[1,6,64,128]{3,2,1,0:T(8,128)} %fusion.229) | copy-start | bytes 589828 | tf_op jit(solution)/shard_map/transpose(jvp())/while
  1129.6 12.7 copy-start.24
  1131.9 27.5 %copy-start.14 = (f32[1,6,64,128]{3,2,1,0:T(8,128)S(1)}, f32[1,6,64,128]{3,2,1,0:T(8,128)}, u32[]{:S(2)}) copy-start(f32[1,6,64,128]{3,2,1,0:T(8,128)} %fusion.229) | copy-start | bytes 589828 | tf_op jit(solution)/shard_map/transpose(jvp())/while
  1174.0 12.7 copy-start.24
  1176.3 27.5 %copy-start.14 = (f32[1,6,64,128]{3,2,1,0:T(8,128)S(1)}, f32[1,6,64,128]{3,2,1,0:T(8,128)}, u32[]{:S(2)}) copy-start(f32[1,6,64,128]{3,2,1,0:T(8,128)} %fusion.229) | copy-start | bytes 589828 | tf_op jit(solution)/shard_map/transpose(jvp())/while
  1218.4 12.7 copy-start.24
  1220.8 27.5 %copy-start.14 = (f32[1,6,64,128]{3,2,1,0:T(8,128)S(1)}, f32[1,6,64,128]{3,2,1,0:T(8,128)}, u32[]{:S(2)}) copy-start(f32[1,6,64,128]{3,2,1,0:T(8,128)} %fusion.229) | copy-start | bytes 589828 | tf_op jit(solution)/shard_map/transpose(jvp())/while
  1262.8 12.7 copy-start.24
  1265.2 27.5 %copy-start.14 = (f32[1,6,64,128]{3,2,1,0:T(8,128)S(1)}, f32[1,6,64,128]{3,2,1,0:T(8,128)}, u32[]{:S(2)}) copy-start(f32[1,6,64,128]{3,2,1,0:T(8,128)} %fusion.229) | copy-start | bytes 589828 | tf_op jit(solution)/shard_map/transpose(jvp())/while
  1307.2 12.7 copy-start.24
  1309.6 27.5 %copy-start.14 = (f32[1,6,64,128]{3,2,1,0:T(8,128)S(1)}, f32[1,6,64,128]{3,2,1,0:T(8,128)}, u32[]{:S(2)}) copy-start(f32[1,6,64,128]{3,2,1,0:T(8,128)} %fusion.229) | copy-start | bytes 589828 | tf_op jit(solution)/shard_map/transpose(jvp())/while
  1354.7 88.3 %all-to-all-start.5 = ((bf16[8,2,768]{2,1,0:T(2,128)(2,1)}), bf16[8,2,768]{2,1,0:T(2,128)(2,1)S(1)}, u32[]{:S(2)}, u32[]{:S(2)}) async-start(bf16[8,2,768]{2,1,0:T(2,128)(2,1)} %reshape.1699), calls=%async_computation.6 | async-start | bytes 49152 | tf_op jit(solution)/shard_map/all_to_all | solution.py:184
  1369.0 12.4 copy-start.41
  1443.0 45.4 %all-to-all-start.4 = ((bf16[8,2,98304]{2,1,0:T(2,128)(2,1)}), bf16[8,2,98304]{2,1,0:T(2,128)(2,1)}, u32[]{:S(2)}, u32[]{:S(2)}) async-start(bf16[8,2,98304]{2,1,0:T(2,128)(2,1)} %reshape.1701), calls=%async_computation.4 | async-start | bytes 6291456 | tf_op jit(solution)/shard_map/all_to_all | solution.py:183
  1447.7 54.6 %reduce-scatter.4.cloned.1.call-start = ((), (), s32[]{:S(2)}) async-start(), calls=%async_computation.12 | async-start | bytes 1179648 | tf_op jit(solution)/shard_map/reduce_scatter | solution.py:186
  1455.5 184.0 %all-reduce.32.cloned.1.call-start = ((), (), s32[]{:S(2)}) async-start(), calls=%async_computation.15 | async-start | bytes 258048 | tf_op jit(solution)/shard_map/psum | solution.py:209
  1458.2 38.1 %copy-start.66 = (f32[3,48]{1,0:T(4,128)}, f32[3,48]{1,0:T(4,128)S(1)}, u32[]{:S(2)}) copy-start(f32[3,48]{1,0:T(4,128)S(1)} %dynamic_update_slice.68) | copy-start | bytes 1732
  1458.8 37.4 %copy-start.20 = (f32[5,3072]{1,0:T(8,128)}, f32[5,3072]{1,0:T(8,128)S(1)}, u32[]{:S(2)}) copy-start(f32[5,3072]{1,0:T(8,128)S(1)} %add_dynamic-update-slice_fusion) | copy-start | bytes 184324
  1502.4 12.6 copy-start.9
  1502.4 12.6 copy-start.25
  1514.9 494.2 %reduce-scatter.6.cloned.1.call-start = ((), (), s32[]{:S(2)}) async-start(), calls=%async_computation.13 | async-start | bytes 41361408 | tf_op jit(solution)/shard_map/reduce_scatter | solution.py:213
  1543.3 96.2 %copy-start.72 = (f32[3,48]{1,0:T(4,128)S(1)}, f32[3,48]{1,0:T(4,128)}, u32[]{:S(2)}) copy-start(f32[3,48]{1,0:T(4,128)} %param.35) | copy-start | bytes 1732
  1543.3 96.2 %copy-start.77 = (f32[3,48]{1,0:T(4,128)S(1)}, f32[3,48]{1,0:T(4,128)}, u32[]{:S(2)}) copy-start(f32[3,48]{1,0:T(4,128)} %param.42) | copy-start | bytes 1732
  1543.3 96.2 %copy-start.78 = (f32[3,48]{1,0:T(4,128)S(1)}, f32[3,48]{1,0:T(4,128)}, u32[]{:S(2)}) copy-start(f32[3,48]{1,0:T(4,128)} %param.49) | copy-start | bytes 1732
  1543.3 98.4 %copy-start.67 = (f32[1536]{0:T(1024)S(1)}, f32[1536]{0:T(1024)}, u32[]{:S(2)}) copy-start(f32[1536]{0:T(1024)} %param.38) | copy-start | bytes 18436
  1543.3 98.4 %copy-start.68 = (f32[1536]{0:T(1024)S(1)}, f32[1536]{0:T(1024)}, u32[]{:S(2)}) copy-start(f32[1536]{0:T(1024)} %param.45) | copy-start | bytes 18436
  1543.3 99.8 %copy-start.37 = (f32[5,256]{1,0:T(8,128)S(1)}, f32[5,256]{1,0:T(8,128)}, u32[]{:S(2)}) copy-start(f32[5,256]{1,0:T(8,128)} %param.34) | copy-start | bytes 15364
  1543.3 99.7 %copy-start.69 = (f32[5,256]{1,0:T(8,128)S(1)}, f32[5,256]{1,0:T(8,128)}, u32[]{:S(2)}) copy-start(f32[5,256]{1,0:T(8,128)} %param.41) | copy-start | bytes 15364
  1543.3 99.7 %copy-start.70 = (f32[5,256]{1,0:T(8,128)S(1)}, f32[5,256]{1,0:T(8,128)}, u32[]{:S(2)}) copy-start(f32[5,256]{1,0:T(8,128)} %param.48) | copy-start | bytes 15364
  1543.3 101.0 %copy-start.50 = (f32[3072]{0:T(1024)S(1)}, f32[3072]{0:T(1024)}, u32[]{:S(2)}) copy-start(f32[3072]{0:T(1024)} %param.39) | copy-start | bytes 36868
  1543.4 101.0 %copy-start.51 = (f32[3072]{0:T(1024)S(1)}, f32[3072]{0:T(1024)}, u32[]{:S(2)}) copy-start(f32[3072]{0:T(1024)} %param.46) | copy-start | bytes 36868
  1543.4 102.4 %copy-start.28 = (f32[5,3072]{1,0:T(8,128)S(1)}, f32[5,3072]{1,0:T(8,128)}, u32[]{:S(2)}) copy-start(f32[5,3072]{1,0:T(8,128)} %param.33) | copy-start | bytes 184324
  1543.4 102.4 %copy-start.31 = (f32[5,3072]{1,0:T(8,128)S(1)}, f32[5,3072]{1,0:T(8,128)}, u32[]{:S(2)}) copy-start(f32[5,3072]{1,0:T(8,128)} %param.40) | copy-start | bytes 184324
  1543.4 102.3 %copy-start.32 = (f32[5,3072]{1,0:T(8,128)S(1)}, f32[5,3072]{1,0:T(8,128)}, u32[]{:S(2)}) copy-start(f32[5,3072]{1,0:T(8,128)} %param.47) | copy-start | bytes 184324
  1543.4 465.7 %copy-start.13 = (f32[48,6448]{1,0:T(8,128)S(1)}, f32[48,6448]{1,0:T(8,128)}, u32[]{:S(2)}) copy-start(f32[48,6448]{1,0:T(8,128)} %param.29) | copy-start | bytes 3714052
  1543.4 465.7 %copy-start.18 = (f32[48,6448]{1,0:T(8,128)S(1)}, f32[48,6448]{1,0:T(8,128)}, u32[]{:S(2)}) copy-start(f32[48,6448]{1,0:T(8,128)} %param.36) | copy-start | bytes 3714052
  1647.4 365.9 %copy-start.35 = (f32[1536]{0:T(1024)S(1)}, f32[1536]{0:T(1024)}, u32[]{:S(2)}) copy-start(f32[1536]{0:T(1024)} %get-tuple-element.1242) | copy-start | bytes 18436
  1647.4 366.5 %copy-start.33 = (f32[3072]{0:T(1024)S(1)}, f32[3072]{0:T(1024)}, u32[]{:S(2)}) copy-start(f32[3072]{0:T(1024)} %get-tuple-element.1243) | copy-start | bytes 36868
  1647.4 367.1 %copy-start.21 = (f32[5,3072]{1,0:T(8,128)S(1)}, f32[5,3072]{1,0:T(8,128)}, u32[]{:S(2)}) copy-start(f32[5,3072]{1,0:T(8,128)} %get-tuple-element.1244) | copy-start | bytes 184324
  1647.4 367.8 %copy-start.34 = (f32[5,256]{1,0:T(8,128)S(1)}, f32[5,256]{1,0:T(8,128)}, u32[]{:S(2)}) copy-start(f32[5,256]{1,0:T(8,128)} %get-tuple-element.1245) | copy-start | bytes 15364
  1647.4 368.4 %copy-start.73 = (f32[3,48]{1,0:T(4,128)S(1)}, f32[3,48]{1,0:T(4,128)}, u32[]{:S(2)}) copy-start(f32[3,48]{1,0:T(4,128)} %get-tuple-element.1246) | copy-start | bytes 1732
  (56 other events, 249.7 us)
Sparse Core Ops, SparseCore 0:
  11.4 132.1 all-gather.3
  159.4 21.6 all-gather.5
  611.0 204.1 reduce-scatter.7
  818.7 80.5 all-gather.7
  1455.6 38.7 reduce-scatter.3
  1515.0 124.3 all-reduce.31
  1646.4 362.6 reduce-scatter.5
where the time goes:
time: 2040 us; the launch traced here: 2020 us
  waiting for transfers between devices  958 us (47%)
  local copies, waits for them, and re-layouts  484 us (24%)
  other arithmetic  326 us (16%)
  matrix products  211 us (10%)
  starting transfers between devices  25.1 us (1%)
    reduce_scatter x1, waiting for transfers between devices, local(): lax.psum_scatter(jnp.einsum('nkm,nkc->mc', column_list, projected_gradien...  362 us
    dynamic_update_slice x56, local copies, waits for them, and re-layouts, state_space(): lax.scan(jax.checkpoint(block_step), start, (blockify(inner), blockify(st...  215 us
    reduce_scatter x1, waiting for transfers between devices, local(): lax.psum_scatter(jnp.einsum('kcb,kch->bh', column_list, cotangent, prefer...  204 us
    all_gather x1, waiting for transfers between devices, local(): lax.all_gather(in_w16, ('seq', 'wshard'), axis=0, tiled=True)  132 us
    unnamed x10, other arithmetic  132 us
    psum x1, waiting for transfers between devices, local(): lax.psum((d_in_gain, d_out_gain, d_conv_full, d_common, d_head_full), ('s...  94.3 us
    another operation x49, other arithmetic  93.2 us
    all_gather x1, waiting for transfers between devices, local(): lax.all_gather(out_w16, ('seq', 'wshard'), axis=0, tiled=True)  76.8 us
  transfers between devices with their start and end apart: 13, of which 9 were waited for; matrix products, arithmetic and copies ran while one was open for 12% of the time, Pallas kernels for 0%

commit v1 on v0

--- a/solution.py
+++ b/solution.py
@@ -15,6 +15,11 @@
 weight_learning_rate = 0.01
 matrix_decay = 0.1
 small_rate = 0.1
+
+
+def swapped_in(x, axis, along):
+    stack = jnp.stack([x] * lax.axis_size(axis))
+    return jnp.concatenate(lax.all_to_all(stack, axis, 0, 0), axis=along)
 
 
 def causal_conv(values, taps):
@@ -127,7 +132,7 @@
     projected = jnp.einsum(
         "fbe,ek->fbk",
         column_list,
-        lax.all_gather(in_w16, ("seq", "wshard"), axis=0, tiled=True),
+        swapped_in(in_w16, ("seq", "wshard"), 0),
         preferred_element_type=jnp.float32,
     ).astype(jnp.bfloat16)
     gate_inner = projected[:, :, : 2 * E]

time: 2040 us -> 2450 us (1.20)
  waiting for transfers between devices: 958 us -> 1270 us
  matrix products: 211 us -> 252 us
  local copies, waits for them, and re-layouts: 484 us -> 520 us
    all_to_all x0 -> x1, waiting for transfers between devices: none -> 430 us  [swapped_in(): return jnp.concatenate(lax.all_to_all(stack, axis, 0, 0), axis=along)]
    all_gather x1, waiting for transfers between devices: 132 us -> 0.01 us  [local(): lax.all_gather(in_w16, ('seq', 'wshard'), axis=0, tiled=True)]
    unnamed x177 -> x183, local copies, waits for them, and re-layouts: 69 us -> 73.3 us
  transfers between devices with their start and end apart: 13 -> 14, of which waited for: 9 -> 9; matrix products, arithmetic and copies ran while one was open for 12% -> 29% of each run, Pallas kernels for 0% -> 0%
where the time goes in v1:
time: 2450 us; the launch traced here: 2440 us
  waiting for transfers between devices  1270 us (52%)
  local copies, waits for them, and re-layouts  520 us (21%)
  other arithmetic  341 us (14%)
  matrix products  252 us (10%)
  starting transfers between devices  33.5 us (1%)
    all_to_all x1, waiting for transfers between devices, swapped_in(): return jnp.concatenate(lax.all_to_all(stack, axis, 0, 0), axis=along)  430 us
    reduce_scatter x1, waiting for transfers between devices, local(): lax.psum_scatter(jnp.einsum('nkm,nkc->mc', column_list, projected_gradien...  362 us
    reduce_scatter x1, waiting for transfers between devices, local(): lax.psum_scatter(jnp.einsum('kcb,kch->bh', column_list, cotangent, prefer...  218 us
    dynamic_update_slice x56, local copies, waits for them, and re-layouts, state_space(): lax.scan(jax.checkpoint(block_step), start, (blockify(inner), blockify(st...  215 us
    unnamed x10, other arithmetic  134 us
    psum x1, waiting for transfers between devices, local(): lax.psum((d_in_gain, d_out_gain, d_conv_full, d_common, d_head_full), ('s...  94.2 us
    another operation x49, other arithmetic  93.2 us
    dot_general x24, matrix products, block_step(): within = jnp.einsum('sijh,sjhp->sihp', weights, inner_part, precision=high)  83.5 us
  transfers between devices with their start and end apart: 14, of which 9 were waited for; matrix products, arithmetic and copies ran while one was open for 29% of the time, Pallas kernels for 0%

profile of v1, /device:TPU:0, one launch (start us, length us, event | category | flops | bytes accessed | tf_op | source)
XLA Modules:
  0.0 2438.2 jit_solution(497407998636934374)
XLA Ops:
  9.4 7.0 stack.2
  16.4 7.4 all-to-all-start
  24.7 429.7 %all-to-all-done = bf16[32,48,6448]{2,1,0:T(8,128)(2,1)} async-done(((bf16[32,48,6448]{2,1,0:T(8,128)(2,1)}), bf16[32,48,6448]{2,1,0:T(8,128)(2,1)}, u32[]{:S(2)}, u32[]{:S(2)}) %all-to-all-start) | async-done | bytes 19808288 | tf_op jit(solution)/shard_map/all_to_all | solution.py:22
  454.5 14.0 fusion.107
  479.5 37.2 %copy.613 = bf16[1,256,6144]{1,0,2:T(2,128)(2,1)} copy(bf16[1,256,6144]{1,2,0:T(8,128)(2,1)S(1)} %slice.200) | data formatting | bytes 6291456 | tf_op jit(solution)/shard_map/slice | solution.py:138
  516.7 31.6 %reduce.89 = bf16[6144,256]{1,0:T(8,128)(2,1)S(1)} reduce(bf16[6144,1,256]{2,1,0:T(2,128)(2,1)} %bitcast.658, bf16[]{:T(256)} %broadcast.1022), dimensions={1}, to_apply=%bitcast.471.reduce_sub_computation | reduce | bytes 6291458
  551.9 4.6 all-to-all-start.2
  571.3 23.1 all-to-all-done.2
  594.3 5.3 reshape.1700
  599.7 9.1 copy.611
  608.7 7.1 reshape.1639
  619.1 4.6 fusion.118
  629.6 192.2 %while.44 = (s32[]{:T(128)}, f32[1,6,64,128]{3,2,1,0:T(8,128)S(1)}, f32[8,1,256,6,64]{2,0,4,3,1:T(8,128)}, f32[8,1,6,64,128]{4,3,2,1,0:T(8,128)}, f32[8,1,256,6]...) while((s32[]{:T(128)}, f32[1,6,64,128]{3,2,1,0:T(8,128)S(1)}, ...), condition=%wide.region_4.5_spmd.clone.clone, body=%wide.region_1.4_spmd.clone.clone.sunk | while | flops 707349504 | bytes 5806421 | solution.py:64
  641.9 9.8 dynamic_update_slice.95
  665.9 9.8 dynamic_update_slice.95
  689.9 9.8 dynamic_update_slice.95
  713.8 9.8 dynamic_update_slice.95
  737.8 9.8 dynamic_update_slice.95
  761.8 9.8 dynamic_update_slice.95
  785.7 9.8 dynamic_update_slice.95
  809.7 9.8 dynamic_update_slice.95
  826.4 4.8 multiply_convert_fusion.1
  831.1 8.5 copy.488
  839.6 35.5 %reduce.90 = bf16[2048,384]{1,0:T(8,128)(2,1)} reduce(bf16[2048,1,384]{2,1,0:T(2,128)(2,1)} %bitcast.670, bf16[]{:T(256)} %broadcast.1022), dimensions={1}, to_apply=%bitcast.433.reduce_sub_computation | reduce | bytes 3145730
  883.2 20.9 all-to-all-done.3
  904.2 6.5 reshape.1702
  919.3 10.7 fusion.139
  930.0 217.9 %reduce-scatter.8.cloned.1.call-done = f32[96,1536]{1,0:T(8,128)} async-done(((f32[3072,1536]{1,0:T(8,128)}), f32[96,1536]{1,0:T(8,128)}) %reduce-scatter.8.cloned.1.call-update) | async-done | bytes 589840 | tf_op jit(solution)/shard_map/reduce_scatter | solution.py:227
  1155.2 76.8 %all-gather.6.cloned.1.call-done = bf16[3072,1536]{1,0:T(8,128)(2,1)} async-done(((bf16[96,1536]{1,0:T(8,128)(2,1)}), bf16[3072,1536]{1,0:T(8,128)(2,1)}) %all-gather.6.cloned.1.call-update) | async-done | bytes 9437200 | tf_op jit(solution)/shard_map/all_gather | solution.py:168
  1232.0 8.4 multiply_reduce_fusion.7
  1242.7 7.6 copy.491
  1250.3 17.8 reduce.91
  1280.5 21.1 all-to-all-done.4
  1301.6 6.3 reshape.1704
  1320.8 433.8 %while.43 = (s32[]{:T(128)}, f32[1,6,64,128]{3,2,1,0:T(8,128)S(1)}, f32[8,1,256,6,64]{2,0,4,3,1:T(8,128)}, f32[8,1,256,6]{3,2,1,0:T(8,128)}, f32[8,1,256,6]{2,0,...) while((s32[]{:T(128)}, f32[1,6,64,128]{3,2,1,0:T(8,128)S(1)}, ...), condition=%wide.region_19.20_spmd.clone, body=%wide.region_7.19_spmd.clone.sunk | while | flops 1670419456 | bytes 15190127 | solution.py:64
  1352.4 7.6 reduce-window.74
  1364.9 9.8 dynamic_update_slice.91
  1406.7 7.5 reduce-window.74
  1419.1 9.8 dynamic_update_slice.91
  1460.9 7.6 reduce-window.74
  1473.3 9.8 dynamic_update_slice.91
  1515.1 7.6 reduce-window.74
  1527.5 9.8 dynamic_update_slice.91
  1569.3 7.6 reduce-window.74
  1581.7 9.8 dynamic_update_slice.91
  1623.5 7.6 reduce-window.74
  1635.9 9.8 dynamic_update_slice.91
  1677.6 7.6 reduce-window.74
  1690.1 9.8 dynamic_update_slice.91
  1731.8 7.6 reduce-window.74
  1744.2 9.8 dynamic_update_slice.91
  1754.6 4.6 transpose.194
  1770.7 13.4 reduce.92
  1790.1 12.1 multiply_reduce_fusion.6
  1806.4 11.3 copy.509
  1817.7 31.7 %reduce.93 = bf16[2048,768]{1,0:T(8,128)(2,1)S(1)} reduce(bf16[2048,1,768]{2,1,0:T(2,128)(2,1)} %bitcast.657, bf16[]{:T(256)} %broadcast.1022), dimensions={1}, to_apply=%bitcast.439.reduce_sub_computation | reduce | bytes 6291458
  1857.8 4.7 all-to-all-start.5
  1875.4 27.8 %all-to-all-done.5 = bf16[8,2,98304]{2,1,0:T(2,128)(2,1)} async-done(((bf16[8,2,98304]{2,1,0:T(2,128)(2,1)}), bf16[8,2,98304]{2,1,0:T(2,128)(2,1)}, u32[]{:S(2)}, u32[]{:S(2)}) %all-to-all-start.5) | async-done | bytes 3145760 | tf_op jit(solution)/shard_map/all_to_all | solution.py:188
  1903.2 7.9 reshape.1708
  1917.2 12.5 fusion.132
  1929.8 18.6 fusion.135
  1950.3 7.8 convert_add_fusion
  1960.0 94.2 %all-reduce.32.cloned.1.call-done = (f32[1536]{0:T(1024)}, f32[3072]{0:T(1024)}, f32[5,3072]{1,0:T(8,128)}, f32[5,256]{1,0:T(8,128)}, f32[3,48]{1,0:T(4,128)}) async-done(((f32[1536]{0:T(1024)}, f32[3072]{0:T(1024)}, f32[5,3072]{1,0:T(8,128)}, f32[5,256]{1,0:T(8,128)}, f32[3,48]{1,0:T(4,128)}), (f32[1536]{0:T(1024)}, f32[3072]{0:T(1024)}, f32[5,3072]{1,0:T(8,128)}, f32[5,256]{1,0:T(8,128)}, ...) | async-done | bytes 85584 | tf_op jit(solution)/shard_map/psum | solution.py:214
  2062.2 361.7 %reduce-scatter.6.cloned.1.call-done = f32[48,6448]{1,0:T(8,128)} async-done(((f32[1536,6448]{1,0:T(8,128)}), f32[48,6448]{1,0:T(8,128)}) %reduce-scatter.6.cloned.1.call-update) | async-done | bytes 1238032 | tf_op jit(solution)/shard_map/reduce_scatter | solution.py:218
  (916 shorter events, 570.7 us)
Async XLA Ops:
  16.4 7.5 copy-start.10
  16.4 438.1 %copy-start.28 = (f32[1536]{0:T(1024)S(1)}, f32[1536]{0:T(1024)}, u32[]{:S(2)}) copy-start(f32[1536]{0:T(1024)} %param.31) | copy-start | bytes 18436
  16.4 438.1 %all-to-all-start = ((bf16[32,48,6448]{2,1,0:T(8,128)(2,1)}), bf16[32,48,6448]{2,1,0:T(8,128)(2,1)}, u32[]{:S(2)}, u32[]{:S(2)}) async-start(bf16[32,48,6448]{2,1,0:T(8,128)(2,1)} %stack.2), calls=%async_computation | async-start | bytes 40108032 | tf_op jit(solution)/shard_map/all_to_all | solution.py:22
  23.9 536.2 %all-gather.4.cloned.1.call-start = ((), (), s32[]{:S(2)}) async-start(), calls=%async_computation.10 | async-start | bytes 1179648 | tf_op jit(solution)/shard_map/all_gather | solution.py:145
  24.7 443.8 %copy-start.50 = (f32[256]{0:T(256)}, f32[256]{0:T(256)S(1)}, u32[]{:S(2)}) copy-start(f32[256]{0:T(256)S(1)} %get-tuple-element.934) | copy-start | bytes 3076
  473.0 78.9 %all-to-all-start.1 = ((bf16[8,2,768]{2,1,0:T(2,128)(2,1)}), bf16[8,2,768]{2,1,0:T(2,128)(2,1)S(1)}, u32[]{:S(2)}, u32[]{:S(2)}) async-start(bf16[8,2,768]{2,1,0:T(2,128)(2,1)} %reshape.1697), calls=%async_computation.1 | async-start | bytes 49152 | tf_op jit(solution)/shard_map/all_to_all | solution.py:143
  551.9 42.4 %all-to-all-start.2 = ((bf16[8,2,98304]{2,1,0:T(2,128)(2,1)}), bf16[8,2,98304]{2,1,0:T(2,128)(2,1)S(1)}, u32[]{:S(2)}, u32[]{:S(2)}) async-start(bf16[8,2,98304]{2,1,0:T(2,128)(2,1)} %reshape.1699), calls=%async_computation.2 | async-start | bytes 6291456 | tf_op jit(solution)/shard_map/all_to_all | solution.py:142
  556.6 8.1 copy-start.64
  556.6 8.1 copy-start.66
  556.8 269.6 %copy-start.48 = (f32[384]{0:T(512)}, f32[384]{0:T(512)S(1)}, u32[]{:S(2)}) copy-start(f32[384]{0:T(512)S(1)} %mul.1143) | copy-start | bytes 4612
  557.8 61.3 %copy-start.40 = (f32[384]{0:T(512)}, f32[384]{0:T(512)S(1)}, u32[]{:S(2)}) copy-start(f32[384]{0:T(512)S(1)} %get-tuple-element.804) | copy-start | bytes 4612
  557.8 61.3 %copy-start.42 = (f32[384]{0:T(512)}, f32[384]{0:T(512)S(1)}, u32[]{:S(2)}) copy-start(f32[384]{0:T(512)S(1)} %get-tuple-element.805) | copy-start | bytes 4612
  557.8 61.3 %copy-start.44 = (f32[384]{0:T(512)}, f32[384]{0:T(512)S(1)}, u32[]{:S(2)}) copy-start(f32[384]{0:T(512)S(1)} %get-tuple-element.806) | copy-start | bytes 4612
  557.8 61.3 %copy-start.46 = (f32[384]{0:T(512)}, f32[384]{0:T(512)S(1)}, u32[]{:S(2)}) copy-start(f32[384]{0:T(512)S(1)} %get-tuple-element.807) | copy-start | bytes 4612
  558.4 6.3 copy-start.60
  558.5 718.2 %copy-start.19 = (bf16[48,1,256]{2,1,0:T(2,128)(2,1)}, bf16[48,1,256]{2,1,0:T(2,128)(2,1)S(1)}, u32[]{:S(2)}) copy-start(bf16[48,1,256]{2,1,0:T(2,128)(2,1)S(1)} %reshape.1698) | copy-start | bytes 73732
  619.1 658.3 %copy-start = (f32[1,2048,6,1,64]{1,4,3,2,0:T(8,128)}, f32[1,2048,6,1,64]{1,4,3,2,0:T(8,128)S(1)}, u32[]{:S(2)}) copy-start(f32[1,2048,6,1,64]{1,4,3,2,0:T(8,128)S(1)} %get-tuple-element.912) | copy-start | bytes 9437188
  875.1 8.1 copy-start.31
  878.9 25.3 %all-to-all-start.3 = ((bf16[8,2,49152]{2,1,0:T(2,128)(2,1)}), bf16[8,2,49152]{2,1,0:T(2,128)(2,1)}, u32[]{:S(2)}, u32[]{:S(2)}) async-start(bf16[8,2,49152]{2,1,0:T(2,128)(2,1)} %reshape.1701), calls=%async_computation.3 | async-start | bytes 3145728 | tf_op jit(solution)/shard_map/all_to_all | solution.py:159
  883.2 264.7 %reduce-scatter.8.cloned.1.call-start = ((), (), s32[]{:S(2)}) async-start(), calls=%async_computation.15 | async-start | bytes 19464192 | tf_op jit(solution)/shard_map/reduce_scatter | solution.py:227
  915.0 325.4 %copy-start.62 = (f32[256]{0:T(256)}, f32[256]{0:T(256)S(1)}, u32[]{:S(2)}) copy-start(f32[256]{0:T(256)S(1)} %get-tuple-element.936) | copy-start | bytes 3076
  930.0 302.0 %all-gather.6.cloned.1.call-start = ((), (), s32[]{:S(2)}) async-start(), calls=%async_computation.11 | async-start | bytes 9732096 | tf_op jit(solution)/shard_map/all_gather | solution.py:168
  1232.0 8.4 copy-start.5
  1271.8 29.8 %all-to-all-start.4 = ((bf16[8,2,49152]{2,1,0:T(2,128)(2,1)}), bf16[8,2,49152]{2,1,0:T(2,128)(2,1)}, u32[]{:S(2)}, u32[]{:S(2)}) async-start(bf16[8,2,49152]{2,1,0:T(2,128)(2,1)} %reshape.1703), calls=%async_computation.4 | async-start | bytes 3145728 | tf_op jit(solution)/shard_map/all_to_all | solution.py:183
  1276.1 641.1 %all-gather.8.cloned.1.call-start = ((), (), s32[]{:S(2)}) async-start(), calls=%async_computation.13 | async-start | bytes 20680704 | tf_op jit(solution)/shard_map/all_gather | solution.py:198
  1766.4 23.7 copy-start.1
  1766.4 23.7 copy-start.49
  1786.5 71.3 %all-to-all-start.6 = ((bf16[8,2,768]{2,1,0:T(2,128)(2,1)}), bf16[8,2,768]{2,1,0:T(2,128)(2,1)S(1)}, u32[]{:S(2)}, u32[]{:S(2)}) async-start(bf16[8,2,768]{2,1,0:T(2,128)(2,1)} %reshape.1705), calls=%async_computation.7 | async-start | bytes 49152 | tf_op jit(solution)/shard_map/all_to_all | solution.py:189
  1790.1 12.2 copy-start.41
  1790.1 12.2 copy-start.43
  1790.1 12.2 copy-start.45
  1790.1 12.2 copy-start.47
  1857.8 45.4 %all-to-all-start.5 = ((bf16[8,2,98304]{2,1,0:T(2,128)(2,1)}), bf16[8,2,98304]{2,1,0:T(2,128)(2,1)}, u32[]{:S(2)}, u32[]{:S(2)}) async-start(bf16[8,2,98304]{2,1,0:T(2,128)(2,1)} %reshape.1707), calls=%async_computation.5 | async-start | bytes 6291456 | tf_op jit(solution)/shard_map/all_to_all | solution.py:188
  1862.5 54.7 %reduce-scatter.4.cloned.1.call-start = ((), (), s32[]{:S(2)}) async-start(), calls=%async_computation.12 | async-start | bytes 1179648 | tf_op jit(solution)/shard_map/reduce_scatter | solution.py:191
  1870.2 184.0 %all-reduce.32.cloned.1.call-start = ((), (), s32[]{:S(2)}) async-start(), calls=%async_computation.16 | async-start | bytes 258048 | tf_op jit(solution)/shard_map/psum | solution.py:214
  1872.9 38.2 %copy-start.68 = (f32[3,48]{1,0:T(4,128)}, f32[3,48]{1,0:T(4,128)S(1)}, u32[]{:S(2)}) copy-start(f32[3,48]{1,0:T(4,128)S(1)} %dynamic_update_slice.68) | copy-start | bytes 1732
  1873.5 37.5 %copy-start.22 = (f32[5,3072]{1,0:T(8,128)}, f32[5,3072]{1,0:T(8,128)S(1)}, u32[]{:S(2)}) copy-start(f32[5,3072]{1,0:T(8,128)S(1)} %add_dynamic-update-slice_fusion) | copy-start | bytes 184324
  1917.2 12.6 copy-start.8
  1917.2 12.6 copy-start.27
  1929.7 494.1 %reduce-scatter.6.cloned.1.call-start = ((), (), s32[]{:S(2)}) async-start(), calls=%async_computation.14 | async-start | bytes 41361408 | tf_op jit(solution)/shard_map/reduce_scatter | solution.py:218
  1950.3 8.0 copy-start.11
  1950.3 8.0 copy-start.15
  1950.3 8.0 copy-start.17
  1950.3 8.0 copy-start.77
  1958.1 96.0 %copy-start.74 = (f32[3,48]{1,0:T(4,128)S(1)}, f32[3,48]{1,0:T(4,128)}, u32[]{:S(2)}) copy-start(f32[3,48]{1,0:T(4,128)} %param.35) | copy-start | bytes 1732
  1958.1 96.0 %copy-start.79 = (f32[3,48]{1,0:T(4,128)S(1)}, f32[3,48]{1,0:T(4,128)}, u32[]{:S(2)}) copy-start(f32[3,48]{1,0:T(4,128)} %param.42) | copy-start | bytes 1732
  1958.2 96.0 %copy-start.80 = (f32[3,48]{1,0:T(4,128)S(1)}, f32[3,48]{1,0:T(4,128)}, u32[]{:S(2)}) copy-start(f32[3,48]{1,0:T(4,128)} %param.49) | copy-start | bytes 1732
  1958.2 98.4 %copy-start.39 = (f32[5,256]{1,0:T(8,128)S(1)}, f32[5,256]{1,0:T(8,128)}, u32[]{:S(2)}) copy-start(f32[5,256]{1,0:T(8,128)} %param.34) | copy-start | bytes 15364
  1958.2 98.4 %copy-start.69 = (f32[5,256]{1,0:T(8,128)S(1)}, f32[5,256]{1,0:T(8,128)}, u32[]{:S(2)}) copy-start(f32[5,256]{1,0:T(8,128)} %param.41) | copy-start | bytes 15364
  1958.2 98.4 %copy-start.70 = (f32[5,256]{1,0:T(8,128)S(1)}, f32[5,256]{1,0:T(8,128)}, u32[]{:S(2)}) copy-start(f32[5,256]{1,0:T(8,128)} %param.48) | copy-start | bytes 15364
  1958.2 99.7 %copy-start.71 = (f32[1536]{0:T(1024)S(1)}, f32[1536]{0:T(1024)}, u32[]{:S(2)}) copy-start(f32[1536]{0:T(1024)} %param.38) | copy-start | bytes 18436
  1958.2 99.7 %copy-start.72 = (f32[1536]{0:T(1024)S(1)}, f32[1536]{0:T(1024)}, u32[]{:S(2)}) copy-start(f32[1536]{0:T(1024)} %param.45) | copy-start | bytes 18436
  1958.2 101.0 %copy-start.52 = (f32[3072]{0:T(1024)S(1)}, f32[3072]{0:T(1024)}, u32[]{:S(2)}) copy-start(f32[3072]{0:T(1024)} %param.39) | copy-start | bytes 36868
  1958.2 101.0 %copy-start.53 = (f32[3072]{0:T(1024)S(1)}, f32[3072]{0:T(1024)}, u32[]{:S(2)}) copy-start(f32[3072]{0:T(1024)} %param.46) | copy-start | bytes 36868
  1958.2 102.3 %copy-start.30 = (f32[5,3072]{1,0:T(8,128)S(1)}, f32[5,3072]{1,0:T(8,128)}, u32[]{:S(2)}) copy-start(f32[5,3072]{1,0:T(8,128)} %param.33) | copy-start | bytes 184324
  1958.2 102.3 %copy-start.33 = (f32[5,3072]{1,0:T(8,128)S(1)}, f32[5,3072]{1,0:T(8,128)}, u32[]{:S(2)}) copy-start(f32[5,3072]{1,0:T(8,128)} %param.40) | copy-start | bytes 184324
  1958.3 102.3 %copy-start.34 = (f32[5,3072]{1,0:T(8,128)S(1)}, f32[5,3072]{1,0:T(8,128)}, u32[]{:S(2)}) copy-start(f32[5,3072]{1,0:T(8,128)} %param.47) | copy-start | bytes 184324
  1958.3 465.6 %copy-start.13 = (f32[48,6448]{1,0:T(8,128)S(1)}, f32[48,6448]{1,0:T(8,128)}, u32[]{:S(2)}) copy-start(f32[48,6448]{1,0:T(8,128)} %param.29) | copy-start | bytes 3714052
  1958.3 465.6 %copy-start.18 = (f32[48,6448]{1,0:T(8,128)S(1)}, f32[48,6448]{1,0:T(8,128)}, u32[]{:S(2)}) copy-start(f32[48,6448]{1,0:T(8,128)} %param.36) | copy-start | bytes 3714052
  2062.2 365.9 %copy-start.37 = (f32[1536]{0:T(1024)S(1)}, f32[1536]{0:T(1024)}, u32[]{:S(2)}) copy-start(f32[1536]{0:T(1024)} %get-tuple-element.1242) | copy-start | bytes 18436
  2062.2 366.5 %copy-start.35 = (f32[3072]{0:T(1024)S(1)}, f32[3072]{0:T(1024)}, u32[]{:S(2)}) copy-start(f32[3072]{0:T(1024)} %get-tuple-element.1243) | copy-start | bytes 36868
  2062.2 367.1 %copy-start.23 = (f32[5,3072]{1,0:T(8,128)S(1)}, f32[5,3072]{1,0:T(8,128)}, u32[]{:S(2)}) copy-start(f32[5,3072]{1,0:T(8,128)} %get-tuple-element.1244) | copy-start | bytes 184324
  2062.2 367.7 %copy-start.36 = (f32[5,256]{1,0:T(8,128)S(1)}, f32[5,256]{1,0:T(8,128)}, u32[]{:S(2)}) copy-start(f32[5,256]{1,0:T(8,128)} %get-tuple-element.1245) | copy-start | bytes 15364
  2062.2 368.3 %copy-start.75 = (f32[3,48]{1,0:T(4,128)S(1)}, f32[3,48]{1,0:T(4,128)}, u32[]{:S(2)}) copy-start(f32[3,48]{1,0:T(4,128)} %get-tuple-element.1246) | copy-start | bytes 1732
  (52 other events, 185.9 us)
Sparse Core Ops, SparseCore 0:
  470.3 36.6 all-gather.3
  930.1 217.7 reduce-scatter.7
  1151.4 80.5 all-gather.5
  1279.4 132.7 all-gather.7
  1870.3 38.6 reduce-scatter.3
  1929.9 124.2 all-reduce.31
  2061.2 362.6 reduce-scatter.5
